TPU v7x, 256 devices: a whole 4x4x8 slice. The times are simulated.
256 devices in a mesh: gx: 16 (over z, core), gy: 16 (over x, y).
Axes of the slice: x: 4, y: 4, z: 8, core: 2. Of those that a mesh axis runs over, the one named last changes fastest.
Arguments:
- earlier_heat_field: float32 [6, 2048, 2048], P(None, 'gx', 'gy'), may hold values from -6 to 6
- substance_per_voxel: int32 [6, 2048, 2048], P(None, 'gx', 'gy'), may hold values from 0 to 7
- patch_wattage_category: int32 [128, 128], P('gx', 'gy'), may hold values from 0 to 63
- planar_coupling: float32 [8], replicated, may hold values from 0.3 to 3
- vertical_coupling_per_substance: float32 [8], replicated, may hold values from 0.05 to 0.5
- heat_mass_ratio: float32 [8], replicated, may hold values from 2e-05 to 0.0002
- wattage_per_category: float32 [64], replicated, may hold values from 2e-06 to 2e-05
Outputs:
- temperature: float32 [6, 2048, 2048], P(None, 'gx', 'gy')
All inputs are finite; a program needn't handle non-finite values.
Results may differ from a plain program's by a relative error of at most 0.0003.
Values sent between devices are 32-bit elements; how exact they have to be, the bound alone decides.
A program may use at most 192 MiB of HBM per device.

v0:
```python
import jax
import jax.numpy as jnp
from jax import lax
from jax.experimental import pallas as pl
from jax.experimental.pallas import tpu as pltpu
from jax.sharding import PartitionSpec as P

MESH = pl.DeviceIdType.MESH
NL = 6
TILE = 16
ITERS = 12
F32 = jnp.float32


class Level:
    def __init__(self, index, block, base, rows, half, whole=False):
        self.index, self.block, self.base, self.rows, self.half, self.whole = index, block, base, rows, half, whole
        self.total = rows + 16
        self.scale = 0.25**index
        step = 24 if rows % 24 == 0 else 16 if rows % 16 == 0 else 8
        self.chunks = [(r, min(step, 8 + rows - r)) for r in range(8, 8 + rows, step)]


def lanes(n):
    return lax.broadcasted_iota(jnp.int32, (n, 128), 1)


def odd(n, k, c):
    bit = lanes(n) & 1
    return bit == 1 if (k + c) % 2 == 0 else bit == 0


def roll(x, shift):
    shift %= 128
    return x if shift == 0 else pltpu.roll(x, shift, 1)


def take(x, index):
    return jnp.take_along_axis(x, index, axis=1, mode="promise_in_bounds")


def thin(x):
    return take(x + roll(x, 127), (2 * lanes(x.shape[0])) & 127)


def wide(x, split=64):
    j = lanes(x.shape[0])
    return take(x, jnp.where(j < split, j >> 1, 64 + (j >> 1)))


def around(refs, t, o, k, r, n, c, pick=()):
    ref = refs[t]
    here = ref[(o, *pick, k, pl.ds(r, n), slice(None))]
    before = ref[(o, *pick, k, pl.ds(r - 1, n), slice(None))]
    after = ref[(o, *pick, k, pl.ds(r + 1, n), slice(None))]
    far = jnp.where(odd(n, k, c), after, before)
    left, right = roll(here, 1), roll(here, 127)
    if len(refs) == 2:
        j = lanes(n)
        beside = refs[1 - t][(o, *pick, k, pl.ds(r, n), slice(None))]
        left = jnp.where(j == 0, roll(beside, 1), left)
        right = jnp.where(j == 127, roll(beside, 127), right)
    return here, far, left, right


def candidate(lv, s, t, c, k, r, n):
    o = 1 - c
    cf = s["cf"][t]
    here, far, left, right = around(s["u"], t, o, k, r, n, c)
    rows = pl.ds(r, n)
    a = cf[c, 0, k, rows, :] * here + cf[c, 1, k, rows, :] * far
    b = cf[c, 2, k, rows, :] * left + cf[c, 3, k, rows, :] * right
    if k > 0:
        a = a + cf[c, 4, k, rows, :] * s["u"][t][o, k - 1, rows, :]
    if k < NL - 1:
        b = b + cf[c, 5, k, rows, :] * s["u"][t][o, k + 1, rows, :]
    return a + b


def half_sweep(lv, s, c):
    for t in range(len(s["u"])):
        for k in range(NL):
            for r, n in lv.chunks:
                rows = pl.ds(r, n)
                s["u"][t][c, k, rows, :] = s["cf"][t][c, 6, k, rows, :] + candidate(lv, s, t, c, k, r, n)


def smooth(lv, s):
    def sweep(i, _):
        half_sweep(lv, s, 0)
        half_sweep(lv, s, 1)
        return 0

    lax.fori_loop(0, 2, sweep, 0)


def residual(lv, s, t, k, r, n):
    rows = pl.ds(r, n)
    parts = []
    for c in (0, 1):
        new = s["cf"][t][c, 6, k, rows, :] + candidate(lv, s, t, c, k, r, n)
        parts.append(s["dg"][t][c, k, rows, :] * (new - s["u"][t][c, k, rows, :]))
    return parts[0] + parts[1]


def inside(lv, t, r, n, gx, gy, nx, ny):
    row = lax.broadcasted_iota(jnp.int32, (n, 128), 0) + (r - lv.base)
    j = lanes(n)
    if lv.whole:
        return (row >= 0) & (row < lv.block * nx // 2) & (j < lv.block * ny)
    half = lv.half // 2
    if lv.index == 0:
        col = j if t == 0 else jnp.where(j < 64, j + 128, j - 128)
    elif lv.index == 1:
        col = jnp.where(j < 96, j, j - 128)
    else:
        col = jnp.where(j < 64, j, j - 128)
    ok = (row >= -half) & (row < lv.block // 2 + half) & (col >= -lv.half) & (col < lv.block + lv.half)
    row, col = row + gx * (lv.block // 2), col + gy * lv.block
    return ok & (row >= 0) & (row < lv.block * nx // 2) & (col >= 0) & (col < lv.block * ny)


def weigh(lv, s, place):
    h = 0.5 * lv.scale
    for t in range(len(s["u"])):
        co = s["co"]
        for r, n in lv.chunks:
            ok = inside(lv, t, r, n, *place)
            rows = pl.ds(r, n)
            for c in (0, 1):
                o = 1 - c
                for k in range(NL):
                    own = co[t][c, 0, k, rows, :]
                    ws = [h * (own + x) for x in around(co, t, o, k, r, n, c, (0,))]
                    diag = co[t][c, 2, k, rows, :] + ((ws[0] + ws[1]) + (ws[2] + ws[3]))
                    mine = co[t][c, 1, k, rows, :]
                    for other, there in ((k - 1, k > 0), (k + 1, k < NL - 1)):
                        if there:
                            face = 0.5 * (mine + co[t][o, 1, other, rows, :])
                            diag = diag + face
                            ws.append(face)
                        else:
                            ws.append(None)
                    inv = jnp.where(ok, 1.0 / diag, 0.0)
                    for i, w in enumerate(ws):
                        if w is not None:
                            s["cf"][t][c, i, k, rows, :] = w * inv
                    s["dg"][t][c, k, rows, :] = diag
                    s["iv"][t][c, k, rows, :] = inv


def pairs(ref, a, start, lv, r, n):
    first = start + 2 * (r - 8)
    even = ref[a, pl.ds(first, n, stride=2), :]
    other = ref[a, pl.ds(first + 1, n, stride=2), :]
    return even, other


def pack_coefficients(lv, s, src, start):
    for m in range(3):
        for k in range(NL):
            for r, n in lv.chunks:
                even, other = pairs(src, m * NL + k, start, lv, r, n)
                for c in (0, 1):
                    s["co"][0][c, m, k, pl.ds(r, n), :] = jnp.where(odd(n, k, c), other, even)


def pack_rhs(lv, s, src, start):
    for k in range(NL):
        for r, n in lv.chunks:
            even, other = pairs(src, k, start, lv, r, n)
            rows = pl.ds(r, n)
            for c in (0, 1):
                f = jnp.where(odd(n, k, c), other, even)
                s["cf"][0][c, 6, k, rows, :] = s["iv"][0][c, k, rows, :] * f


def restrict_rhs(lv, s, dst):
    for k in range(NL):
        for r, n in lv.chunks:
            dst[k, pl.ds(r, n), :] = 0.25 * thin(residual(lv, s, 0, k, r, n))


def restrict_coefficients(lv, s, dst):
    for m in range(3):
        for k in range(NL):
            for r, n in lv.chunks:
                rows = pl.ds(r, n)
                dst[m * NL + k, rows, :] = 0.25 * thin(s["co"][0][0, m, k, rows, :] + s["co"][0][1, m, k, rows, :])


def spread(lv, s, dst):
    for k in range(NL):
        for r, n in lv.chunks:
            red, black = s["u"][0][0, k, pl.ds(r, n), :], s["u"][0][1, k, pl.ds(r, n), :]
            m = odd(n, k, 0)
            dst[k, pl.ds(2 * r, n, stride=2), :] = jnp.where(m, black, red)
            dst[k, pl.ds(2 * r + 1, n, stride=2), :] = jnp.where(m, red, black)


def correct(lv, s, src, start):
    for k in range(NL):
        for r, n in lv.chunks:
            x = src[k, pl.ds(start + r - 8, n), :]
            rows = pl.ds(r, n)
            for t in range(len(s["u"])):
                if lv.index > 0:
                    add = wide(x, 96 if lv.index == 1 else 64)
                else:
                    j = lanes(n)
                    add = take(x, (j >> 1) + 64 * t)
                for c in (0, 1):
                    s["u"][t][c, k, rows, :] = s["u"][t][c, k, rows, :] + add


def choose(label, entries):
    b0, b1, b2 = (label & 1) == 1, (label & 2) == 2, (label & 4) == 4
    low = [jnp.where(b0, entries[i + 1], entries[i]) for i in (0, 2, 4, 6)]
    return jnp.where(b2, jnp.where(b1, low[3], low[2]), jnp.where(b1, low[1], low[0]))


def clear_margins(lv, s):
    for t in range(len(s["u"])):
        for r in (0, 8 + lv.rows):
            zero = jnp.zeros((8, 128), F32)
            for c in (0, 1):
                for k in range(NL):
                    s["u"][t][c, k, pl.ds(r, 8), :] = zero
                    s["co"][t][c, 0, k, pl.ds(r, 8), :] = zero


def clear(lv, s):
    for k in range(NL):
        for r, n in lv.chunks:
            for c in (0, 1):
                s["u"][0][c, k, pl.ds(r, n), :] = jnp.zeros((n, 128), F32)


def coarse_solve(lv, s, r_ref, e_ref):
    u, cf, dg, iv = s["u"][0], s["cf"][0], s["dg"][0], s["iv"][0]
    cells = [(c, k, r, n) for c in (0, 1) for k in range(NL) for r, n in lv.chunks]

    def total(parts):
        while len(parts) > 1:
            parts = [a + b for a, b in zip(parts[::2], parts[1::2])] + ([parts[-1]] if len(parts) % 2 else [])
        return jnp.sum(jnp.sum(parts[0], axis=0, keepdims=True), axis=1, keepdims=True)

    parts = []
    for c, k, r, n in cells:
        rows = pl.ds(r, n)
        z = cf[c, 6, k, rows, :]
        f = dg[c, k, rows, :] * z
        u[c, k, rows, :] = z
        r_ref[c, k, rows, :] = f
        e_ref[c, k, rows, :] = jnp.zeros_like(f)
        parts.append(f * z)

    def step(i, inner):
        images, parts = [], []
        for c, k, r, n in cells:
            rows = pl.ds(r, n)
            search = u[c, k, rows, :]
            image = dg[c, k, rows, :] * (search - candidate(lv, s, 0, c, k, r, n))
            images.append(image)
            parts.append(search * image)
        alpha = inner / total(parts)
        parts = []
        for (c, k, r, n), image in zip(cells, images):
            rows = pl.ds(r, n)
            e_ref[c, k, rows, :] = e_ref[c, k, rows, :] + alpha * u[c, k, rows, :]
            left = r_ref[c, k, rows, :] - alpha * image
            r_ref[c, k, rows, :] = left
            parts.append(left * (left * iv[c, k, rows, :]))
        after = total(parts)
        beta = after / inner
        for c, k, r, n in cells:
            rows = pl.ds(r, n)
            u[c, k, rows, :] = r_ref[c, k, rows, :] * iv[c, k, rows, :] + beta * u[c, k, rows, :]
        return after

    lax.fori_loop(0, ITERS, step, total(parts))
    for c, k, r, n in cells:
        rows = pl.ds(r, n)
        u[c, k, rows, :] = e_ref[c, k, rows, :]


def halve(src, dst, arrays, rows):
    step = min(rows, 32)

    def one(a, _):
        for r in range(0, rows, step):
            even = src[a, pl.ds(2 * r, step, stride=2), :]
            other = src[a, pl.ds(2 * r + 1, step, stride=2), :]
            dst[a, pl.ds(r, step), :] = 0.25 * thin(even + other)
        return 0

    lax.fori_loop(0, arrays, one, 0)


def kernel(nx, ny, levels, heat_field, substance, category, planar, vertical, mass, wattage, out, *scratch):
    gx, gy = lax.axis_index("gx"), lax.axis_index("gy")
    place = (gx, gy, nx, ny)
    it = iter(scratch)
    st = []
    for lv in levels:
        tiles = 2 if lv.index == 0 else 1
        st.append({name: [next(it) for _ in range(tiles)] for name in ("u", "cf", "dg", "iv", "co")})
    ui, uh, cu0, cu1, cu2, cu3, cu4, cu5 = (next(it) for _ in range(8))
    f1, f3, f5, c1, c3, c5, sr, sp, cr, ce = (next(it) for _ in range(10))
    m0, k0, r0, q0 = (next(it) for _ in range(4))
    mc1, kc1, rc1, qc1, nc1 = (next(it) for _ in range(5))
    mf1, kf1, rf1, qf1, nf1 = (next(it) for _ in range(5))
    rr_c1, rr_f1 = next(it), next(it)
    b3c, g3c, b3f, g3f = (next(it) for _ in range(4))
    a5c, h5c, d5c, l5c = (next(it) for _ in range(4))
    a5f, h5f, d5f, l5f = (next(it) for _ in range(4))
    s0, s1c, s1f, s3c, s3f, s5c, s5f, s6c, s6f = (next(it) for _ in range(9))

    def exists(dx, dy):
        return (gx + dx >= 0) & (gx + dx < nx) & (gy + dy >= 0) & (gy + dy < ny)

    barrier = pltpu.get_barrier_semaphore()

    def greet_near(q, _):
        dx, dy = q // 5 - 2, lax.rem(q, 5) - 2

        @pl.when(exists(dx, dy) & (dx != 0) & (dy != 0))
        def _():
            pl.semaphore_signal(barrier, inc=1, device_id={"gx": gx + dx, "gy": gy + dy}, device_id_type=MESH)

        return 0

    lax.fori_loop(0, 25, greet_near, 0)

    def greet_gx(d, _):
        @pl.when(d != gx)
        def _():
            pl.semaphore_signal(barrier, inc=1, device_id={"gx": d}, device_id_type=MESH)

        return 0

    def greet_gy(d, _):
        @pl.when(d != gy)
        def _():
            pl.semaphore_signal(barrier, inc=1, device_id={"gy": d}, device_id_type=MESH)

        return 0

    lax.fori_loop(0, nx, greet_gx, 0)
    lax.fori_loop(0, ny, greet_gy, 0)

    def reach(at, size):
        return jnp.minimum(at, 2) + jnp.minimum(size - 1 - at, 2)

    for k in range(NL):
        for r in range(0, 128, 32):
            ui[k, pl.ds(8 + r, 32), :] = heat_field[k, pl.ds(r, 32), :]
            ui[NL + k, pl.ds(8 + r, 32), :] = substance[k, pl.ds(r, 32), :].astype(F32)
    for i in range(8):
        row = jnp.zeros((8, 128), F32)
        for jj in range(8):
            row = jnp.where((lanes(8) >> 4) == jj, wattage[category[i, jj]], row)
        ui[12, pl.ds(8 + 16 * i, 8), :] = row
        ui[12, pl.ds(16 + 16 * i, 8), :] = row

    def columns0(a, _):
        first, last = jnp.zeros((8, 128), F32), jnp.zeros((8, 128), F32)
        slot = lanes(8) >> 3
        for g in range(16):
            z = roll(ui[a, pl.ds(8 + 8 * g, 8), :], 8 * g)
            first = jnp.where(slot == g, z, first)
            last = jnp.where(slot == (g + 15) % 16, z, last)
        m0[0, a] = first
        m0[1, a] = last
        return 0

    lax.fori_loop(0, 13, columns0, 0)
    slot8 = lanes(8) >> 3
    for i, r in ((0, 8), (1, 128)):
        first, last = jnp.zeros((8, 128), F32), jnp.zeros((8, 128), F32)
        for a in range(13):
            z = roll(ui[a, pl.ds(r, 8), :], 8 * a)
            first = jnp.where(slot8 == a, z, first)
            last = jnp.where(slot8 == (a + 15) % 16, z, last)
        k0[2 * i] = first
        k0[2 * i + 1] = last

    pl.semaphore_wait(barrier, (nx - 1) + (ny - 1) + reach(gx, nx) * reach(gy, ny))

    SIDES = [(-1, 0), (1, 0), (0, -1), (0, 1), (-1, -1), (-1, 1), (1, -1), (1, 1)]

    def side_copy(i, src, dst, sems):
        dx, dy = SIDES[i]
        opposite = SIDES.index((-dx, -dy))
        return pltpu.make_async_remote_copy(
            src_ref=src, dst_ref=dst, send_sem=sems.at[0, i], recv_sem=sems.at[1, opposite],
            device_id={"gx": gx + dx, "gy": gy + dy}, device_id_type=MESH,
        )

    def sides(refs, sems, action):
        for i, (dx, dy) in enumerate(SIDES):
            @pl.when(exists(dx, dy))
            def _(i=i):
                copy = side_copy(i, refs[i][0], refs[i][1], sems)
                if action == "start":
                    copy.start()
                elif action == "sent":
                    copy.wait_send()

    def arrive(refs, sems):
        for i, (dx, dy) in enumerate(SIDES):
            opposite = SIDES.index((-dx, -dy))

            @pl.when(exists(dx, dy))
            def _(opposite=opposite):
                side_copy(opposite, refs[opposite][0], refs[opposite][1], sems).wait_recv()

    def absent(fills):
        for (dx, dy), ref in zip(SIDES, fills):
            @pl.when(jnp.logical_not(exists(dx, dy)))
            def _(ref=ref):
                ref[...] = jnp.zeros(ref.shape, F32)

    top, bottom = pl.ds(0, 8), pl.ds(136, 8)
    ex0 = [
        (ui.at[:, pl.ds(8, 8), :], ui.at[:, bottom, :]),
        (ui.at[:, pl.ds(128, 8), :], ui.at[:, top, :]),
        (m0.at[0], r0.at[1]),
        (m0.at[1], r0.at[0]),
        (k0.at[0], q0.at[3]),
        (k0.at[1], q0.at[2]),
        (k0.at[2], q0.at[1]),
        (k0.at[3], q0.at[0]),
    ]
    sides(ex0, s0, "start")
    absent([ui.at[:, top, :], ui.at[:, bottom, :], r0.at[0], r0.at[1], q0.at[0], q0.at[1], q0.at[2], q0.at[3]])

    tables = [[ref[i] for i in range(8)] for ref in (planar, vertical, mass)]

    def own(k, _):
        for r in range(0, 128, 16):
            label = substance[k, pl.ds(r, 16), :]
            for m in range(3):
                cu0[m * NL + k, pl.ds(r, 16), :] = choose(label, tables[m])
        return 0

    lax.fori_loop(0, NL, own, 0)
    cu4[...] = jnp.zeros(cu4.shape, F32)
    halve(cu0, cu1, 18, 64)
    halve(cu1, cu2, 18, 32)
    halve(cu2, cu3, 18, 16)
    halve(cu3, cu4, 18, 8)
    halve(cu4, cu5, 18, 8)

    def pack1(src, arrays, m, k, rws):
        slot = lanes(8) >> 5

        def one(a, _):
            for v in range(2):
                first, last = jnp.zeros((8, 128), F32), jnp.zeros((8, 128), F32)
                for q in range(4):
                    z = roll(src[a, pl.ds(32 * v + 8 * q, 8), :], 32 * q)
                    first = jnp.where(slot == q, z, first)
                    last = jnp.where(slot == (q + 1) % 4, z, last)
                m[0, a, pl.ds(8 * v, 8), :] = first
                m[1, a, pl.ds(8 * v, 8), :] = last
                k[2 * v, a] = first
                k[2 * v + 1, a] = last
                x = src[a, pl.ds(32 * v, 16), :]
                y = src[a, pl.ds(32 * v + 16, 16), :]
                rws[v, a] = jnp.where(lanes(16) < 64, x, roll(y, 64))
            return 0

        lax.fori_loop(0, arrays, one, 0)

    def exchange1(m, k, rws, r, q, n):
        return [
            (rws.at[0], n.at[1]), (rws.at[1], n.at[0]),
            (m.at[0], r.at[1]), (m.at[1], r.at[0]),
            (k.at[0], q.at[3]), (k.at[1], q.at[2]), (k.at[2], q.at[1]), (k.at[3], q.at[0]),
        ]

    def absent1(r, q, n):
        absent([n.at[0], n.at[1], r.at[0], r.at[1], q.at[0], q.at[1], q.at[2], q.at[3]])

    def unpack1(src, dst, arrays, r, q, n):
        slot, j8 = lanes(8) >> 5, lanes(8)

        def one(a, _):
            for v in range(2):
                own_rows, over = n[v, a], roll(n[v, a], 64)
                for g in range(4):
                    z = roll(jnp.where(slot == g, q[2 * v + 1, a], q[2 * v, a]), 64 - 32 * g)
                    x = (own_rows if g < 2 else over)[8 * (g % 2) : 8 * (g % 2) + 8]
                    dst[a, pl.ds(96 * v + 8 * g, 8), :] = jnp.where(j8 < 64, x, z)
                    y = roll(jnp.where(slot == g, r[1, a, pl.ds(8 * v, 8), :], r[0, a, pl.ds(8 * v, 8), :]), 64 - 32 * g)
                    x = src[a, pl.ds(32 * v + 8 * g, 8), :]
                    dst[a, pl.ds(32 + 32 * v + 8 * g, 8), :] = jnp.where(j8 < 64, x, y)
            return 0

        lax.fori_loop(0, arrays, one, 0)

    pack1(cu1, 18, mc1, kc1, rr_c1)
    exc1 = exchange1(mc1, kc1, rr_c1, rc1, qc1, nc1)
    sides(exc1, s1c, "start")
    absent1(rc1, qc1, nc1)

    def pack3(src, sets, dst):
        for m in range(sets):
            total = src[m * NL, pl.ds(0, 16), :]
            for k in range(1, NL):
                z = roll(src[m * NL + k, pl.ds(0, 16), :], 16 * k)
                total = jnp.where((lanes(16) >> 4) == k, z, total)
            dst[m] = total

    def near(action, src, dst, sems):
        def one(q, _):
            dx, dy = q // 5 - 2, lax.rem(q, 5) - 2

            @pl.when(exists(dx, dy) & (q != 12))
            def _():
                there = 24 - q
                if action == "arrive":
                    pltpu.make_async_remote_copy(
                        src_ref=src, dst_ref=dst.at[q], send_sem=sems.at[0, there], recv_sem=sems.at[1, q],
                        device_id={"gx": gx + dx, "gy": gy + dy}, device_id_type=MESH,
                    ).wait_recv()
                else:
                    copy = pltpu.make_async_remote_copy(
                        src_ref=src, dst_ref=dst.at[there], send_sem=sems.at[0, q], recv_sem=sems.at[1, there],
                        device_id={"gx": gx + dx, "gy": gy + dy}, device_id_type=MESH,
                    )
                    if action == "start":
                        copy.start()
                    else:
                        copy.wait_send()

            if action == "start":
                @pl.when(jnp.logical_not(exists(dx, dy)))
                def _():
                    dst[q] = jnp.zeros(dst.shape[1:], F32)

            return 0

        lax.fori_loop(0, 25, one, 0)

    def unpack3(src, got, sets, dst):
        j = lanes(16)
        slot = j >> 4
        for m in range(sets):
            def rows(x, _, m=m):
                for k in range(NL):
                    total = jnp.zeros((16, 128), F32)
                    for dy in range(-2, 3):
                        z = roll(got[x * 5 + dy + 2, m], 16 * dy - 16 * k)
                        total = jnp.where(slot == dy % 8, z, total)
                    dst[m * NL + k, pl.ds(pl.multiple_of(16 * x, 16), 16), :] = total
                return 0

            lax.fori_loop(0, 5, rows, 0)

    pack3(cu3, 3, b3c)
    near("start", b3c, g3c, s3c)
    g3c[12] = b3c[...]

    def pack5(src, arrays, dst):
        total = src[0, pl.ds(0, 8), :]
        for a in range(1, arrays):
            total = jnp.where((lanes(8) >> 2) == a, roll(src[a, pl.ds(0, 8), :], 4 * a), total)
        dst[...] = total

    def line(action, axis, me, size, src, dst, sems):
        def one(d, _):
            @pl.when(d != me)
            def _():
                if action == "arrive":
                    pltpu.make_async_remote_copy(
                        src_ref=src, dst_ref=dst.at[d], send_sem=sems.at[0, d], recv_sem=sems.at[1, d],
                        device_id={axis: d}, device_id_type=MESH,
                    ).wait_recv()
                else:
                    copy = pltpu.make_async_remote_copy(
                        src_ref=src, dst_ref=dst.at[me], send_sem=sems.at[0, d], recv_sem=sems.at[1, me],
                        device_id={axis: d}, device_id_type=MESH,
                    )
                    if action == "start":
                        copy.start()
                    else:
                        copy.wait_send()

            return 0

        lax.fori_loop(0, size, one, 0)

    def strip5(got, arrays, dst):
        j8 = lanes(8)
        low = lax.broadcasted_iota(jnp.int32, (8, 128), 0) < 4
        strips = []
        for a in range(arrays):
            total = jnp.zeros((8, 128), F32)
            for d in range(ny):
                total = jnp.where((j8 >> 2) == d, roll(got[d], 4 * d - 4 * a), total)
            strips.append(total)
        for t in range((arrays + 3) // 4):
            four = [strips[a] if a < arrays else jnp.zeros((8, 128), F32) for a in range(4 * t, 4 * t + 4)]
            x = jnp.where(j8 < 64, four[0], roll(four[1], 64))
            y = jnp.where(j8 < 64, four[2], roll(four[3], 64))
            dst[pl.ds(8 * t, 8), :] = jnp.where(low, x, pltpu.roll(y, 4, 0))

    def whole5(got, arrays, dst):
        j8 = lanes(8)
        low = lax.broadcasted_iota(jnp.int32, (8, 128), 0) < 4
        for a in range(arrays):
            t, up, right = a // 4, (a // 2) % 2, a % 2
            for h in range(nx // 2):
                x, y = got[2 * h, pl.ds(8 * t, 8), :], got[2 * h + 1, pl.ds(8 * t, 8), :]
                if up == 0:
                    y = pltpu.roll(y, 4, 0)
                else:
                    x = pltpu.roll(x, 4, 0)
                z = jnp.where(low, x, y)
                dst[a, pl.ds(8 * h, 8), :] = jnp.where(j8 < 64, roll(z, 64 * right), 0.0)

    pack5(cu5, 18, a5c)
    line("start", "gy", gy, ny, a5c, h5c, s5c)
    h5c[gy] = a5c[...]

    for lv, s in zip(levels, st):
        clear_margins(lv, s)
    for lv, s in list(zip(levels, st))[1:6]:
        clear(lv, s)
    for ref in (sr, sp):
        ref[...] = jnp.zeros(ref.shape, F32)

    arrive(ex0, s0)

    def beside0(a, _):
        slot = lanes(8) >> 3
        for g in range(16):
            uh[a, pl.ds(8 + 8 * g, 8), :] = roll(jnp.where(slot == g, r0[1, a], r0[0, a]), -8 * g)
        return 0

    lax.fori_loop(0, 13, beside0, 0)
    for i, r in ((0, 0), (1, 136)):
        for a in range(13):
            uh[a, pl.ds(r, 8), :] = roll(jnp.where(slot8 == a, q0[2 * i + 1], q0[2 * i]), -8 * a)

    lv, s = levels[0], st[0]
    for t, src in enumerate((ui, uh)):
        for r, n in lv.chunks:
            ok = inside(lv, t, r, n, *place)
            rows = pl.ds(r, n)
            for k in range(NL):
                label = pairs(src, NL + k, 0, lv, r, n)
                value = pairs(src, k, 0, lv, r, n)
                for c in (0, 1):
                    m = odd(n, k, c)
                    kind = jnp.where(m, label[1], label[0]).astype(jnp.int32)
                    s["u"][t][c, k, rows, :] = jnp.where(m, value[1], value[0])
                    s["co"][t][c, 0, k, rows, :] = jnp.where(ok, choose(kind, tables[0]), 0.0)
                    s["co"][t][c, 1, k, rows, :] = choose(kind, tables[1])
                    s["co"][t][c, 2, k, rows, :] = choose(kind, tables[2])
    weigh(lv, s, place)
    for t, src in enumerate((ui, uh)):
        for r, n in lv.chunks:
            rows = pl.ds(r, n)
            heat = pairs(src, 12, 0, lv, r, n)
            for k in range(NL):
                for c in (0, 1):
                    f = s["co"][t][c, 2, k, rows, :] * s["u"][t][c, k, rows, :]
                    if k == 0:
                        f = f + jnp.where(odd(n, k, c), heat[1], heat[0])
                    s["cf"][t][c, 6, k, rows, :] = s["iv"][t][c, k, rows, :] * f
    smooth(lv, s)
    restrict_rhs(lv, s, sr)
    for k in range(NL):
        for r in range(0, 64, 32):
            f5[k, pl.ds(r, 32), :] = sr[k, pl.ds(lv.base + r, 32), :]
    pack1(f5, 6, mf1, kf1, rr_f1)
    exf1 = exchange1(mf1, kf1, rr_f1, rf1, qf1, nf1)
    sides(exf1, s1f, "start")
    absent1(rf1, qf1, nf1)

    line("arrive", "gy", gy, ny, a5c, h5c, s5c)
    strip5(h5c, 18, d5c)
    arrive(exc1, s1c)
    unpack1(cu1, c1, 18, rc1, qc1, nc1)
    line("start", "gx", gx, nx, d5c, l5c, s6c)
    l5c[gx] = d5c[...]
    pack_coefficients(levels[1], st[1], c1, 0)
    weigh(levels[1], st[1], place)
    c1[...] = jnp.zeros(c1.shape, F32)
    restrict_coefficients(levels[1], st[1], c1)
    pack_coefficients(levels[2], st[2], c1, levels[1].base + 2 * (8 - levels[2].base))
    weigh(levels[2], st[2], place)

    arrive(exf1, s1f)
    unpack1(f5, f1, 6, rf1, qf1, nf1)
    pack_rhs(levels[1], st[1], f1, 0)
    smooth(levels[1], st[1])
    restrict_rhs(levels[1], st[1], sr)
    pack_rhs(levels[2], st[2], sr, levels[1].base + 2 * (8 - levels[2].base))
    smooth(levels[2], st[2])
    restrict_rhs(levels[2], st[2], sr)
    for k in range(NL):
        f3[k, pl.ds(0, 16), :] = sr[k, pl.ds(levels[2].base, 16), :]
    pack3(f3, 1, b3f)
    near("arrive", b3c, g3c, s3c)
    near("start", b3f, g3f, s3f)
    g3f[12] = b3f[...]
    unpack3(b3c, g3c, 3, c3)
    pack_coefficients(levels[3], st[3], c3, 0)
    weigh(levels[3], st[3], place)
    c1[...] = jnp.zeros(c1.shape, F32)
    restrict_coefficients(levels[3], st[3], c1)
    pack_coefficients(levels[4], st[4], c1, levels[3].base + 2 * (8 - levels[4].base))
    weigh(levels[4], st[4], place)
    sr[...] = jnp.zeros(sr.shape, F32)

    near("arrive", b3f, g3f, s3f)
    unpack3(b3f, g3f, 1, f3)
    pack_rhs(levels[3], st[3], f3, 0)
    smooth(levels[3], st[3])
    restrict_rhs(levels[3], st[3], sr)
    pack_rhs(levels[4], st[4], sr, levels[3].base + 2 * (8 - levels[4].base))
    smooth(levels[4], st[4])
    restrict_rhs(levels[4], st[4], sr)
    for k in range(NL):
        cu5[k, pl.ds(0, 8), :] = sr[k, pl.ds(levels[4].base, 8), :]
    pack5(cu5, 6, a5f)
    line("arrive", "gx", gx, nx, d5c, l5c, s6c)
    line("start", "gy", gy, ny, a5f, h5f, s5f)
    h5f[gy] = a5f[...]

    whole5(l5c, 18, c5)
    pack_coefficients(levels[5], st[5], c5, 0)
    weigh(levels[5], st[5], place)
    line("arrive", "gy", gy, ny, a5f, h5f, s5f)
    strip5(h5f, 6, d5f)
    c1[...] = jnp.zeros(c1.shape, F32)
    line("start", "gx", gx, nx, d5f, l5f, s6f)
    l5f[gx] = d5f[...]
    restrict_coefficients(levels[5], st[5], c1)
    pack_coefficients(levels[6], st[6], c1, 8)
    weigh(levels[6], st[6], place)
    sr[...] = jnp.zeros(sr.shape, F32)
    line("arrive", "gx", gx, nx, d5f, l5f, s6f)
    whole5(l5f, 6, f5)
    pack_rhs(levels[5], st[5], f5, 0)
    smooth(levels[5], st[5])
    restrict_rhs(levels[5], st[5], sr)
    pack_rhs(levels[6], st[6], sr, 8)
    coarse_solve(levels[6], st[6], cr, ce)

    sp[...] = jnp.zeros(sp.shape, F32)
    spread(levels[6], st[6], sp)
    correct(levels[5], st[5], sp, 2 * levels[6].base + 8 - levels[5].base)
    smooth(levels[5], st[5])
    sp[...] = jnp.zeros(sp.shape, F32)
    spread(levels[5], st[5], sp)
    lv, s = levels[4], st[4]
    first = 2 * levels[5].base + 8 - lv.base + 4 * gx
    for k in range(NL):
        x = sp[k, pl.ds(first, lv.rows), :]
        add = wide(pltpu.roll(x, lax.rem(128 - 4 * gy, 128), 1))
        for c in (0, 1):
            rows = pl.ds(8, lv.rows)
            s["u"][0][c, k, rows, :] = s["u"][0][c, k, rows, :] + add
    smooth(lv, s)
    for i in (3, 2, 1, 0):
        sp[...] = jnp.zeros(sp.shape, F32)
        spread(levels[i + 1], st[i + 1], sp)
        correct(levels[i], st[i], sp, 2 * levels[i + 1].base + 8 - levels[i].base)
        smooth(levels[i], st[i])
    u = st[0]["u"][0]
    for k in range(NL):
        for r in range(0, 64, 32):
            red, black = u[0, k, pl.ds(levels[0].base + r, 32), :], u[1, k, pl.ds(levels[0].base + r, 32), :]
            m = odd(32, k, 0)
            out[k, pl.ds(2 * r, 32, stride=2), :] = jnp.where(m, black, red)
            out[k, pl.ds(2 * r + 1, 32, stride=2), :] = jnp.where(m, red, black)

    sides(ex0, s0, "sent")
    sides(exc1, s1c, "sent")
    sides(exf1, s1f, "sent")
    near("sent", b3c, g3c, s3c)
    near("sent", b3f, g3f, s3f)
    line("sent", "gy", gy, ny, a5c, h5c, s5c)
    line("sent", "gy", gy, ny, a5f, h5f, s5f)
    line("sent", "gx", gx, nx, d5c, l5c, s6c)
    line("sent", "gx", gx, nx, d5f, l5f, s6f)


def solution(mesh):
    nx, ny = mesh.shape["gx"], mesh.shape["gy"]
    levels = [
        Level(0, 128, 12, 72, 8),
        Level(1, 64, 24, 64, 32),
        Level(2, 32, 16, 32, 16),
        Level(3, 16, 24, 40, 32),
        Level(4, 8, 16, 24, 16),
        Level(5, 4, 8, 2 * nx, 0, True),
        Level(6, 2, 8, max(8, nx), 0, True),
    ]

    def buffer(*shape):
        return pltpu.VMEM(shape, F32)

    scratch = []
    for lv in levels:
        tiles = 2 if lv.index == 0 else 1
        n = lv.total
        for shape in ((2, 6, n, 128), (2, 7, 6, n, 128), (2, 6, n, 128), (2, 6, n, 128), (2, 3, 6, n, 128)):
            scratch += [buffer(*shape)] * tiles
    scratch += [buffer(13, 144, 128)] * 2
    scratch += [buffer(18, n, 128) for n in (128, 64, 32, 16, 16, 8)]
    scratch += [buffer(6, 128, 128), buffer(6, 80, 128), buffer(6, max(64, 4 * nx), 128)]
    scratch += [buffer(18, 128, 128), buffer(18, 80, 128), buffer(18, 4 * nx, 128)]
    scratch += [buffer(6, 96, 128), buffer(6, 160, 128)]
    n = levels[6].total
    scratch += [buffer(2, 6, n, 128)] * 2
    scratch += [buffer(2, 13, 8, 128), buffer(4, 8, 128), buffer(2, 13, 8, 128), buffer(4, 8, 128)]
    for a in (18, 6):
        scratch += [buffer(2, a, 16, 128), buffer(4, a, 8, 128), buffer(2, a, 16, 128), buffer(4, a, 8, 128), buffer(2, a, 16, 128)]
    scratch += [buffer(2, 18, 16, 128), buffer(2, 6, 16, 128)]
    scratch += [buffer(3, 16, 128), buffer(25, 3, 16, 128), buffer(1, 16, 128), buffer(25, 1, 16, 128)]
    for rows in (40, 16):
        scratch += [buffer(8, 128), buffer(ny, 8, 128), buffer(rows, 128), buffer(nx, rows, 128)]
    scratch += [pltpu.SemaphoreType.DMA((2, 8))] * 3 + [pltpu.SemaphoreType.DMA((2, 25))] * 2
    scratch += [pltpu.SemaphoreType.DMA((2, ny))] * 2 + [pltpu.SemaphoreType.DMA((2, nx))] * 2

    def on_device(*args):
        vmem, smem = pl.BlockSpec(memory_space=pltpu.VMEM), pl.BlockSpec(memory_space=pltpu.SMEM)

        def body(*refs):
            kernel(nx, ny, levels, *refs)

        return pl.pallas_call(
            body,
            out_shape=jax.ShapeDtypeStruct((6, 128, 128), F32),
            in_specs=[vmem, vmem] + [smem] * 5,
            out_specs=vmem,
            scratch_shapes=scratch,
            compiler_params=pltpu.CompilerParams(
                collective_id=0, has_side_effects=True, vmem_limit_bytes=60 * 2**20
            ),
            name="vcycle",
        )(*args)

    placed = (P(None, "gx", "gy"), P(None, "gx", "gy"), P("gx", "gy"), P(), P(), P(), P())
    return jax.shard_map(on_device, mesh=mesh, in_specs=placed, out_specs=P(None, "gx", "gy"), check_vma=False)
```

profile of v0, /device:TPU:1, one launch (start us, length us, event | category | flops | bytes accessed | tf_op | source)
XLA Modules:
  0.0 94.4 jit_solution(7573621990903113832)
XLA Ops:
  0.0 92.6 %vcycle.1 = f32[6,128,128]{2,1,0:T(8,128)} custom-call(f32[6,128,128]{2,1,0:T(8,128)} %refs_0_.1, s32[6,128,128]{2,1,0:T(8,128)} %refs_1_.1, s32[8,8]{1,0:T(8,128)} %refs_2_.1, f32[8]{0:T(128)} %refs_3_.1, f32[8]{0:T(128)} %refs_4_.1, f32[8]{0:T(128)} %refs_5_.1, f32[64]{0:T(128)} %refs_6_.1), custom_call_target="tpu_custom_call" | custom-call | tf_op jit(solution)/shard_map/vcycle/pallas_call | solution.py:838
  92.6 1.8 %copy.9 = f32[6,128,128]{2,1,0:T(8,128)} copy(f32[6,128,128]{2,1,0:T(8,128)} %vcycle.1) | data formatting | bytes 786432
where the time goes:
time: 94.5 us; the launch traced here: 94.4 us
  Pallas kernels  92.6 us (98%)
  local copies, waits for them, and re-layouts  1.77 us (2%)
    pallas_call x1, Pallas kernels, on_device(): pl.pallas_call(body, out_shape=jax.ShapeDtypeStruct((6, 128, 128), F32),...  92.6 us

commit v1 on v0

--- a/solution.py
+++ b/solution.py
@@ -39,8 +39,13 @@
     return jnp.take_along_axis(x, index, axis=1, mode="promise_in_bounds")
 
 
-def thin(x):
-    return take(x + roll(x, 127), (2 * lanes(x.shape[0])) & 127)
+def thin(ref, spots):
+    for a, r, n in spots:
+        x = ref[a, pl.ds(r, n), :]
+        ref[a, pl.ds(r, n), :] = 0.25 * (x + roll(x, 127))
+    for a, r, n in spots:
+        x = ref[a, pl.ds(r, n), :]
+        ref[a, pl.ds(r, n), :] = take(x, (2 * lanes(n)) & 127)
 
 
 def wide(x, split=64):
@@ -178,7 +183,8 @@
 def restrict_rhs(lv, s, dst):
     for k in range(NL):
         for r, n in lv.chunks:
-            dst[k, pl.ds(r, n), :] = 0.25 * thin(residual(lv, s, 0, k, r, n))
+            dst[k, pl.ds(r, n), :] = residual(lv, s, 0, k, r, n)
+    thin(dst, [(k, r, n) for k in range(NL) for r, n in lv.chunks])
 
 
 def restrict_coefficients(lv, s, dst):
@@ -186,7 +192,8 @@
         for k in range(NL):
             for r, n in lv.chunks:
                 rows = pl.ds(r, n)
-                dst[m * NL + k, rows, :] = 0.25 * thin(s["co"][0][0, m, k, rows, :] + s["co"][0][1, m, k, rows, :])
+                dst[m * NL + k, rows, :] = s["co"][0][0, m, k, rows, :] + s["co"][0][1, m, k, rows, :]
+    thin(dst, [(a, r, n) for a in range(3 * NL) for r, n in lv.chunks])
 
 
 def spread(lv, s, dst):
@@ -236,7 +243,7 @@
                 s["u"][0][c, k, pl.ds(r, n), :] = jnp.zeros((n, 128), F32)
 
 
-def coarse_solve(lv, s, r_ref, e_ref):
+def coarse_solve(lv, s, r_ref, p_ref, q_ref, e_ref):
     u, cf, dg, iv = s["u"][0], s["cf"][0], s["dg"][0], s["iv"][0]
     cells = [(c, k, r, n) for c in (0, 1) for k in range(NL) for r, n in lv.chunks]
 
@@ -245,68 +252,71 @@
             parts = [a + b for a, b in zip(parts[::2], parts[1::2])] + ([parts[-1]] if len(parts) % 2 else [])
         return jnp.sum(jnp.sum(parts[0], axis=0, keepdims=True), axis=1, keepdims=True)
 
-    parts = []
+    def images():
+        ws, rz, zw = [], [], []
+        for c, k, r, n in cells:
+            rows = pl.ds(r, n)
+            z = u[c, k, rows, :]
+            w = dg[c, k, rows, :] * (z - candidate(lv, s, 0, c, k, r, n))
+            ws.append(w)
+            rz.append(r_ref[c, k, rows, :] * z)
+            zw.append(z * w)
+        return ws, total(rz), total(zw)
+
     for c, k, r, n in cells:
         rows = pl.ds(r, n)
         z = cf[c, 6, k, rows, :]
-        f = dg[c, k, rows, :] * z
         u[c, k, rows, :] = z
-        r_ref[c, k, rows, :] = f
-        e_ref[c, k, rows, :] = jnp.zeros_like(f)
-        parts.append(f * z)
-
-    def step(i, inner):
-        images, parts = [], []
+        r_ref[c, k, rows, :] = dg[c, k, rows, :] * z
+    ws, rz, zw = images()
+    for (c, k, r, n), w in zip(cells, ws):
+        rows = pl.ds(r, n)
+        p_ref[c, k, rows, :] = u[c, k, rows, :]
+        q_ref[c, k, rows, :] = w
+        e_ref[c, k, rows, :] = jnp.zeros_like(w)
+
+    def step(i, carry):
+        rz, alpha = carry
         for c, k, r, n in cells:
             rows = pl.ds(r, n)
-            search = u[c, k, rows, :]
-            image = dg[c, k, rows, :] * (search - candidate(lv, s, 0, c, k, r, n))
-            images.append(image)
-            parts.append(search * image)
-        alpha = inner / total(parts)
-        parts = []
-        for (c, k, r, n), image in zip(cells, images):
+            left = r_ref[c, k, rows, :] - alpha * q_ref[c, k, rows, :]
+            r_ref[c, k, rows, :] = left
+            u[c, k, rows, :] = left * iv[c, k, rows, :]
+            e_ref[c, k, rows, :] = e_ref[c, k, rows, :] + alpha * p_ref[c, k, rows, :]
+        ws, after, zw = images()
+        beta = after / rz
+        for (c, k, r, n), w in zip(cells, ws):
             rows = pl.ds(r, n)
-            e_ref[c, k, rows, :] = e_ref[c, k, rows, :] + alpha * u[c, k, rows, :]
-            left = r_ref[c, k, rows, :] - alpha * image
-            r_ref[c, k, rows, :] = left
-            parts.append(left * (left * iv[c, k, rows, :]))
-        after = total(parts)
-        beta = after / inner
-        for c, k, r, n in cells:
-            rows = pl.ds(r, n)
-            u[c, k, rows, :] = r_ref[c, k, rows, :] * iv[c, k, rows, :] + beta * u[c, k, rows, :]
-        return after
-
-    lax.fori_loop(0, ITERS, step, total(parts))
+            p_ref[c, k, rows, :] = u[c, k, rows, :] + beta * p_ref[c, k, rows, :]
+            q_ref[c, k, rows, :] = w + beta * q_ref[c, k, rows, :]
+        return after, after / (zw - beta * after / alpha)
+
+    rz, alpha = lax.fori_loop(0, ITERS - 1, step, (rz, rz / zw))
     for c, k, r, n in cells:
         rows = pl.ds(r, n)
-        u[c, k, rows, :] = e_ref[c, k, rows, :]
+        u[c, k, rows, :] = e_ref[c, k, rows, :] + alpha * p_ref[c, k, rows, :]
 
 
 def halve(src, dst, arrays, rows):
     step = min(rows, 32)
-
-    def one(a, _):
-        for r in range(0, rows, step):
-            even = src[a, pl.ds(2 * r, step, stride=2), :]
-            other = src[a, pl.ds(2 * r + 1, step, stride=2), :]
-            dst[a, pl.ds(r, step), :] = 0.25 * thin(even + other)
-        return 0
-
-    lax.fori_loop(0, arrays, one, 0)
+    spots = [(a, r, step) for a in range(arrays) for r in range(0, rows, step)]
+    for a, r, n in spots:
+        dst[a, pl.ds(r, n), :] = src[a, pl.ds(2 * r, n, stride=2), :] + src[a, pl.ds(2 * r + 1, n, stride=2), :]
+    thin(dst, spots)
 
 
 def kernel(nx, ny, levels, heat_field, substance, category, planar, vertical, mass, wattage, out, *scratch):
     gx, gy = lax.axis_index("gx"), lax.axis_index("gy")
     place = (gx, gy, nx, ny)
+    half, core = nx // 2, lax.rem(gx, 2)
+    at5 = core * half + gx // 2
     it = iter(scratch)
     st = []
     for lv in levels:
         tiles = 2 if lv.index == 0 else 1
         st.append({name: [next(it) for _ in range(tiles)] for name in ("u", "cf", "dg", "iv", "co")})
     ui, uh, cu0, cu1, cu2, cu3, cu4, cu5 = (next(it) for _ in range(8))
-    f1, f3, f5, c1, c3, c5, sr, sp, cr, ce = (next(it) for _ in range(10))
+    f1, f3, f5, c1, c3, c5, sr, sp, cr, cp, cq, ce = (next(it) for _ in range(12))
     m0, k0, r0, q0 = (next(it) for _ in range(4))
     mc1, kc1, rc1, qc1, nc1 = (next(it) for _ in range(5))
     mf1, kf1, rf1, qf1, nf1 = (next(it) for _ in range(5))
@@ -314,40 +324,27 @@
     b3c, g3c, b3f, g3f = (next(it) for _ in range(4))
     a5c, h5c, d5c, l5c = (next(it) for _ in range(4))
     a5f, h5f, d5f, l5f = (next(it) for _ in range(4))
-    s0, s1c, s1f, s3c, s3f, s5c, s5f, s6c, s6f = (next(it) for _ in range(9))
+    s0, s1c, s1f, s3c, s3f, s5c, s5f, s6c, s6f, s7c = (next(it) for _ in range(10))
 
     def exists(dx, dy):
         return (gx + dx >= 0) & (gx + dx < nx) & (gy + dy >= 0) & (gy + dy < ny)
 
+    for q in range(25):
+        if q != 12:
+            g3c[q] = jnp.zeros(g3c.shape[1:], F32)
+            g3f[q] = jnp.zeros(g3f.shape[1:], F32)
     barrier = pltpu.get_barrier_semaphore()
 
-    def greet_near(q, _):
-        dx, dy = q // 5 - 2, lax.rem(q, 5) - 2
-
-        @pl.when(exists(dx, dy) & (dx != 0) & (dy != 0))
-        def _():
-            pl.semaphore_signal(barrier, inc=1, device_id={"gx": gx + dx, "gy": gy + dy}, device_id_type=MESH)
-
-        return 0
-
-    lax.fori_loop(0, 25, greet_near, 0)
-
-    def greet_gx(d, _):
-        @pl.when(d != gx)
-        def _():
-            pl.semaphore_signal(barrier, inc=1, device_id={"gx": d}, device_id_type=MESH)
-
-        return 0
-
-    def greet_gy(d, _):
-        @pl.when(d != gy)
-        def _():
-            pl.semaphore_signal(barrier, inc=1, device_id={"gy": d}, device_id_type=MESH)
-
-        return 0
-
-    lax.fori_loop(0, nx, greet_gx, 0)
-    lax.fori_loop(0, ny, greet_gy, 0)
+    def greet(**where):
+        pl.semaphore_signal(barrier, inc=1, device_id=where, device_id_type=MESH)
+
+    for dx in (-2, -1, 1, 2):
+        for dy in (-2, -1, 1, 2):
+            pl.when(exists(dx, dy))(lambda dx=dx, dy=dy: greet(gx=gx + dx, gy=gy + dy))
+    for d in range(1, nx):
+        greet(gx=lax.rem(gx + d, nx))
+    for d in range(1, ny):
+        greet(gy=lax.rem(gy + d, ny))
 
     def reach(at, size):
         return jnp.minimum(at, 2) + jnp.minimum(size - 1 - at, 2)
@@ -363,7 +360,7 @@
         ui[12, pl.ds(8 + 16 * i, 8), :] = row
         ui[12, pl.ds(16 + 16 * i, 8), :] = row
 
-    def columns0(a, _):
+    for a in range(13):
         first, last = jnp.zeros((8, 128), F32), jnp.zeros((8, 128), F32)
         slot = lanes(8) >> 3
         for g in range(16):
@@ -372,9 +369,6 @@
             last = jnp.where(slot == (g + 15) % 16, z, last)
         m0[0, a] = first
         m0[1, a] = last
-        return 0
-
-    lax.fori_loop(0, 13, columns0, 0)
     slot8 = lanes(8) >> 3
     for i, r in ((0, 8), (1, 128)):
         first, last = jnp.zeros((8, 128), F32), jnp.zeros((8, 128), F32)
@@ -384,6 +378,19 @@
             last = jnp.where(slot8 == (a + 15) % 16, z, last)
         k0[2 * i] = first
         k0[2 * i + 1] = last
+
+    tables = [[ref[i] for i in range(8)] for ref in (planar, vertical, mass)]
+
+    def own(k, _):
+        for r in range(0, 128, 16):
+            label = substance[k, pl.ds(r, 16), :]
+            for m in range(3):
+                cu0[m * NL + k, pl.ds(r, 16), :] = choose(label, tables[m])
+        return 0
+
+    lax.fori_loop(0, NL, own, 0)
+    cu4[...] = jnp.zeros(cu4.shape, F32)
+    halve(cu0, cu1, 18, 64)
 
     pl.semaphore_wait(barrier, (nx - 1) + (ny - 1) + reach(gx, nx) * reach(gy, ny))
 
@@ -435,28 +442,11 @@
     sides(ex0, s0, "start")
     absent([ui.at[:, top, :], ui.at[:, bottom, :], r0.at[0], r0.at[1], q0.at[0], q0.at[1], q0.at[2], q0.at[3]])
 
-    tables = [[ref[i] for i in range(8)] for ref in (planar, vertical, mass)]
-
-    def own(k, _):
-        for r in range(0, 128, 16):
-            label = substance[k, pl.ds(r, 16), :]
-            for m in range(3):
-                cu0[m * NL + k, pl.ds(r, 16), :] = choose(label, tables[m])
-        return 0
-
-    lax.fori_loop(0, NL, own, 0)
-    cu4[...] = jnp.zeros(cu4.shape, F32)
-    halve(cu0, cu1, 18, 64)
-    halve(cu1, cu2, 18, 32)
-    halve(cu2, cu3, 18, 16)
-    halve(cu3, cu4, 18, 8)
-    halve(cu4, cu5, 18, 8)
-
     def pack1(src, arrays, m, k, rws):
         slot = lanes(8) >> 5
 
-        def one(a, _):
-            for v in range(2):
+        def one(i, _):
+            for a, v in [(3 * i + e, v) for e in range(3) for v in range(2)]:
                 first, last = jnp.zeros((8, 128), F32), jnp.zeros((8, 128), F32)
                 for q in range(4):
                     z = roll(src[a, pl.ds(32 * v + 8 * q, 8), :], 32 * q)
@@ -471,7 +461,7 @@
                 rws[v, a] = jnp.where(lanes(16) < 64, x, roll(y, 64))
             return 0
 
-        lax.fori_loop(0, arrays, one, 0)
+        lax.fori_loop(0, arrays // 3, one, 0)
 
     def exchange1(m, k, rws, r, q, n):
         return [
@@ -486,8 +476,8 @@
     def unpack1(src, dst, arrays, r, q, n):
         slot, j8 = lanes(8) >> 5, lanes(8)
 
-        def one(a, _):
-            for v in range(2):
+        def one(i, _):
+            for a, v in [(3 * i + e, v) for e in range(3) for v in range(2)]:
                 own_rows, over = n[v, a], roll(n[v, a], 64)
                 for g in range(4):
                     z = roll(jnp.where(slot == g, q[2 * v + 1, a], q[2 * v, a]), 64 - 32 * g)
@@ -498,12 +488,7 @@
                     dst[a, pl.ds(32 + 32 * v + 8 * g, 8), :] = jnp.where(j8 < 64, x, y)
             return 0
 
-        lax.fori_loop(0, arrays, one, 0)
-
-    pack1(cu1, 18, mc1, kc1, rr_c1)
-    exc1 = exchange1(mc1, kc1, rr_c1, rc1, qc1, nc1)
-    sides(exc1, s1c, "start")
-    absent1(rc1, qc1, nc1)
+        lax.fori_loop(0, arrays // 3, one, 0)
 
     def pack3(src, sets, dst):
         for m in range(sets):
@@ -514,54 +499,36 @@
             dst[m] = total
 
     def near(action, src, dst, sems):
-        def one(q, _):
-            dx, dy = q // 5 - 2, lax.rem(q, 5) - 2
-
-            @pl.when(exists(dx, dy) & (q != 12))
-            def _():
-                there = 24 - q
-                if action == "arrive":
+        if action == "start":
+            for q in [q for q in range(25) if q != 12]:
+                dx, dy = q // 5 - 2, q % 5 - 2
+
+                @pl.when(exists(dx, dy))
+                def _(dx=dx, dy=dy, q=q):
                     pltpu.make_async_remote_copy(
-                        src_ref=src, dst_ref=dst.at[q], send_sem=sems.at[0, there], recv_sem=sems.at[1, q],
+                        src_ref=src, dst_ref=dst.at[24 - q], send_sem=sems.at[0], recv_sem=sems.at[1],
                         device_id={"gx": gx + dx, "gy": gy + dy}, device_id_type=MESH,
-                    ).wait_recv()
-                else:
-                    copy = pltpu.make_async_remote_copy(
-                        src_ref=src, dst_ref=dst.at[there], send_sem=sems.at[0, q], recv_sem=sems.at[1, there],
-                        device_id={"gx": gx + dx, "gy": gy + dy}, device_id_type=MESH,
-                    )
-                    if action == "start":
-                        copy.start()
-                    else:
-                        copy.wait_send()
-
-            if action == "start":
-                @pl.when(jnp.logical_not(exists(dx, dy)))
-                def _():
-                    dst[q] = jnp.zeros(dst.shape[1:], F32)
-
-            return 0
-
-        lax.fori_loop(0, 25, one, 0)
+                    ).start()
+
+            return
+        for a in (2, 3, 4):
+            for b in (2, 3, 4):
+                @pl.when((reach(gx, nx) == a) & (reach(gy, ny) == b))
+                def _(count=(a + 1) * (b + 1) - 1):
+                    part = dst.at[pl.ds(0, count)]
+                    pltpu.make_async_copy(part, part, sems.at[1 if action == "arrive" else 0]).wait()
 
     def unpack3(src, got, sets, dst):
         j = lanes(16)
         slot = j >> 4
         for m in range(sets):
-            def rows(x, _, m=m):
+            for x in range(5):
                 for k in range(NL):
                     total = jnp.zeros((16, 128), F32)
                     for dy in range(-2, 3):
                         z = roll(got[x * 5 + dy + 2, m], 16 * dy - 16 * k)
                         total = jnp.where(slot == dy % 8, z, total)
-                    dst[m * NL + k, pl.ds(pl.multiple_of(16 * x, 16), 16), :] = total
-                return 0
-
-            lax.fori_loop(0, 5, rows, 0)
-
-    pack3(cu3, 3, b3c)
-    near("start", b3c, g3c, s3c)
-    g3c[12] = b3c[...]
+                    dst[m * NL + k, pl.ds(16 * x, 16), :] = total
 
     def pack5(src, arrays, dst):
         total = src[0, pl.ds(0, 8), :]
@@ -570,27 +537,15 @@
         dst[...] = total
 
     def line(action, axis, me, size, src, dst, sems):
-        def one(d, _):
-            @pl.when(d != me)
-            def _():
-                if action == "arrive":
-                    pltpu.make_async_remote_copy(
-                        src_ref=src, dst_ref=dst.at[d], send_sem=sems.at[0, d], recv_sem=sems.at[1, d],
-                        device_id={axis: d}, device_id_type=MESH,
-                    ).wait_recv()
-                else:
-                    copy = pltpu.make_async_remote_copy(
-                        src_ref=src, dst_ref=dst.at[me], send_sem=sems.at[0, d], recv_sem=sems.at[1, me],
-                        device_id={axis: d}, device_id_type=MESH,
-                    )
-                    if action == "start":
-                        copy.start()
-                    else:
-                        copy.wait_send()
-
-            return 0
-
-        lax.fori_loop(0, size, one, 0)
+        if action == "start":
+            for d in range(1, size):
+                pltpu.make_async_remote_copy(
+                    src_ref=src, dst_ref=dst.at[me], send_sem=sems.at[0], recv_sem=sems.at[1],
+                    device_id={axis: lax.rem(me + d, size)}, device_id_type=MESH,
+                ).start()
+            return
+        part = dst.at[pl.ds(0, size - 1)]
+        pltpu.make_async_copy(part, part, sems.at[1 if action == "arrive" else 0]).wait()
 
     def strip5(got, arrays, dst):
         j8 = lanes(8)
@@ -607,13 +562,13 @@
             y = jnp.where(j8 < 64, four[2], roll(four[3], 64))
             dst[pl.ds(8 * t, 8), :] = jnp.where(low, x, pltpu.roll(y, 4, 0))
 
-    def whole5(got, arrays, dst):
+    def whole5(got, arrays, dst, order):
         j8 = lanes(8)
         low = lax.broadcasted_iota(jnp.int32, (8, 128), 0) < 4
         for a in range(arrays):
             t, up, right = a // 4, (a // 2) % 2, a % 2
             for h in range(nx // 2):
-                x, y = got[2 * h, pl.ds(8 * t, 8), :], got[2 * h + 1, pl.ds(8 * t, 8), :]
+                x, y = got[order(2 * h), pl.ds(8 * t, 8), :], got[order(2 * h + 1), pl.ds(8 * t, 8), :]
                 if up == 0:
                     y = pltpu.roll(y, 4, 0)
                 else:
@@ -621,7 +576,16 @@
                 z = jnp.where(low, x, y)
                 dst[a, pl.ds(8 * h, 8), :] = jnp.where(j8 < 64, roll(z, 64 * right), 0.0)
 
+    exc1 = exchange1(mc1, kc1, rr_c1, rc1, qc1, nc1)
+    pack1(cu1, 18, mc1, kc1, rr_c1)
+    halve(cu1, cu2, 18, 32)
+    sides(exc1, s1c, "start")
+    halve(cu2, cu3, 18, 16)
+    halve(cu3, cu4, 18, 8)
+    halve(cu4, cu5, 18, 8)
     pack5(cu5, 18, a5c)
+    pack3(cu3, 3, b3c)
+    absent1(rc1, qc1, nc1)
     line("start", "gy", gy, ny, a5c, h5c, s5c)
     h5c[gy] = a5c[...]
 
@@ -629,18 +593,15 @@
         clear_margins(lv, s)
     for lv, s in list(zip(levels, st))[1:6]:
         clear(lv, s)
-    for ref in (sr, sp):
-        ref[...] = jnp.zeros(ref.shape, F32)
+    for k in range(NL):
+        for r in (8, 80, 88):
+            sp[k, pl.ds(r, 8), :] = jnp.zeros((8, 128), F32)
 
     arrive(ex0, s0)
 
-    def beside0(a, _):
-        slot = lanes(8) >> 3
+    for a in range(13):
         for g in range(16):
-            uh[a, pl.ds(8 + 8 * g, 8), :] = roll(jnp.where(slot == g, r0[1, a], r0[0, a]), -8 * g)
-        return 0
-
-    lax.fori_loop(0, 13, beside0, 0)
+            uh[a, pl.ds(8 + 8 * g, 8), :] = roll(jnp.where(slot8 == g, r0[1, a], r0[0, a]), -8 * g)
     for i, r in ((0, 0), (1, 136)):
         for a in range(13):
             uh[a, pl.ds(r, 8), :] = roll(jnp.where(slot8 == a, q0[2 * i + 1], q0[2 * i]), -8 * a)
@@ -679,20 +640,25 @@
     pack1(f5, 6, mf1, kf1, rr_f1)
     exf1 = exchange1(mf1, kf1, rr_f1, rf1, qf1, nf1)
     sides(exf1, s1f, "start")
+    g3c[12] = b3c[...]
     absent1(rf1, qf1, nf1)
 
+    arrive(exc1, s1c)
+    unpack1(cu1, c1, 18, rc1, qc1, nc1)
     line("arrive", "gy", gy, ny, a5c, h5c, s5c)
     strip5(h5c, 18, d5c)
-    arrive(exc1, s1c)
-    unpack1(cu1, c1, 18, rc1, qc1, nc1)
-    line("start", "gx", gx, nx, d5c, l5c, s6c)
-    l5c[gx] = d5c[...]
+    l5c[at5] = d5c[...]
+    for d in range(1, half):
+        pltpu.make_async_remote_copy(
+            src_ref=d5c, dst_ref=l5c.at[at5], send_sem=s6c.at[0], recv_sem=s6c.at[1],
+            device_id={"gx": lax.rem(gx + 2 * d, nx)}, device_id_type=MESH,
+        ).start()
     pack_coefficients(levels[1], st[1], c1, 0)
     weigh(levels[1], st[1], place)
-    c1[...] = jnp.zeros(c1.shape, F32)
     restrict_coefficients(levels[1], st[1], c1)
     pack_coefficients(levels[2], st[2], c1, levels[1].base + 2 * (8 - levels[2].base))
     weigh(levels[2], st[2], place)
+    near("start", b3c, g3c, s3c)
 
     arrive(exf1, s1f)
     unpack1(f5, f1, 6, rf1, qf1, nf1)
@@ -707,15 +673,22 @@
     pack3(f3, 1, b3f)
     near("arrive", b3c, g3c, s3c)
     near("start", b3f, g3f, s3f)
+    strips = l5c.at[pl.ds(0, half - 1)]
+    pltpu.make_async_copy(strips, strips, s6c.at[1]).wait()
+    pltpu.make_async_copy(strips, strips, s6c.at[0]).wait()
+    mine = l5c.at[pl.ds(core * half, half)]
+    relay = pltpu.make_async_remote_copy(
+        src_ref=mine, dst_ref=mine, send_sem=s7c.at[0], recv_sem=s7c.at[1],
+        device_id={"gx": gx + 1 - 2 * core}, device_id_type=MESH,
+    )
+    relay.start()
     g3f[12] = b3f[...]
     unpack3(b3c, g3c, 3, c3)
     pack_coefficients(levels[3], st[3], c3, 0)
     weigh(levels[3], st[3], place)
-    c1[...] = jnp.zeros(c1.shape, F32)
     restrict_coefficients(levels[3], st[3], c1)
     pack_coefficients(levels[4], st[4], c1, levels[3].base + 2 * (8 - levels[4].base))
     weigh(levels[4], st[4], place)
-    sr[...] = jnp.zeros(sr.shape, F32)
 
     near("arrive", b3f, g3f, s3f)
     unpack3(b3f, g3f, 1, f3)
@@ -728,35 +701,39 @@
     for k in range(NL):
         cu5[k, pl.ds(0, 8), :] = sr[k, pl.ds(levels[4].base, 8), :]
     pack5(cu5, 6, a5f)
-    line("arrive", "gx", gx, nx, d5c, l5c, s6c)
     line("start", "gy", gy, ny, a5f, h5f, s5f)
     h5f[gy] = a5f[...]
-
-    whole5(l5c, 18, c5)
+    relay.wait_recv()
+
+    whole5(l5c, 18, c5, lambda g: g % 2 * half + g // 2)
     pack_coefficients(levels[5], st[5], c5, 0)
     weigh(levels[5], st[5], place)
     line("arrive", "gy", gy, ny, a5f, h5f, s5f)
     strip5(h5f, 6, d5f)
-    c1[...] = jnp.zeros(c1.shape, F32)
     line("start", "gx", gx, nx, d5f, l5f, s6f)
     l5f[gx] = d5f[...]
     restrict_coefficients(levels[5], st[5], c1)
     pack_coefficients(levels[6], st[6], c1, 8)
     weigh(levels[6], st[6], place)
-    sr[...] = jnp.zeros(sr.shape, F32)
+    sides(ex0, s0, "sent")
+    sides(exc1, s1c, "sent")
+    sides(exf1, s1f, "sent")
+    near("sent", b3c, g3c, s3c)
+    near("sent", b3f, g3f, s3f)
+    line("sent", "gy", gy, ny, a5c, h5c, s5c)
+    line("sent", "gy", gy, ny, a5f, h5f, s5f)
+    relay.wait_send()
     line("arrive", "gx", gx, nx, d5f, l5f, s6f)
-    whole5(l5f, 6, f5)
+    whole5(l5f, 6, f5, lambda g: g)
     pack_rhs(levels[5], st[5], f5, 0)
     smooth(levels[5], st[5])
     restrict_rhs(levels[5], st[5], sr)
     pack_rhs(levels[6], st[6], sr, 8)
-    coarse_solve(levels[6], st[6], cr, ce)
-
-    sp[...] = jnp.zeros(sp.shape, F32)
+    coarse_solve(levels[6], st[6], cr, cp, cq, ce)
+
     spread(levels[6], st[6], sp)
     correct(levels[5], st[5], sp, 2 * levels[6].base + 8 - levels[5].base)
     smooth(levels[5], st[5])
-    sp[...] = jnp.zeros(sp.shape, F32)
     spread(levels[5], st[5], sp)
     lv, s = levels[4], st[4]
     first = 2 * levels[5].base + 8 - lv.base + 4 * gx
@@ -768,7 +745,6 @@
             s["u"][0][c, k, rows, :] = s["u"][0][c, k, rows, :] + add
     smooth(lv, s)
     for i in (3, 2, 1, 0):
-        sp[...] = jnp.zeros(sp.shape, F32)
         spread(levels[i + 1], st[i + 1], sp)
         correct(levels[i], st[i], sp, 2 * levels[i + 1].base + 8 - levels[i].base)
         smooth(levels[i], st[i])
@@ -780,14 +756,6 @@
             out[k, pl.ds(2 * r, 32, stride=2), :] = jnp.where(m, black, red)
             out[k, pl.ds(2 * r + 1, 32, stride=2), :] = jnp.where(m, red, black)
 
-    sides(ex0, s0, "sent")
-    sides(exc1, s1c, "sent")
-    sides(exf1, s1f, "sent")
-    near("sent", b3c, g3c, s3c)
-    near("sent", b3f, g3f, s3f)
-    line("sent", "gy", gy, ny, a5c, h5c, s5c)
-    line("sent", "gy", gy, ny, a5f, h5f, s5f)
-    line("sent", "gx", gx, nx, d5c, l5c, s6c)
     line("sent", "gx", gx, nx, d5f, l5f, s6f)
 
 
@@ -818,7 +786,7 @@
     scratch += [buffer(18, 128, 128), buffer(18, 80, 128), buffer(18, 4 * nx, 128)]
     scratch += [buffer(6, 96, 128), buffer(6, 160, 128)]
     n = levels[6].total
-    scratch += [buffer(2, 6, n, 128)] * 2
+    scratch += [buffer(2, 6, n, 128)] * 4
     scratch += [buffer(2, 13, 8, 128), buffer(4, 8, 128), buffer(2, 13, 8, 128), buffer(4, 8, 128)]
     for a in (18, 6):
         scratch += [buffer(2, a, 16, 128), buffer(4, a, 8, 128), buffer(2, a, 16, 128), buffer(4, a, 8, 128), buffer(2, a, 16, 128)]
@@ -826,8 +794,7 @@
     scratch += [buffer(3, 16, 128), buffer(25, 3, 16, 128), buffer(1, 16, 128), buffer(25, 1, 16, 128)]
     for rows in (40, 16):
         scratch += [buffer(8, 128), buffer(ny, 8, 128), buffer(rows, 128), buffer(nx, rows, 128)]
-    scratch += [pltpu.SemaphoreType.DMA((2, 8))] * 3 + [pltpu.SemaphoreType.DMA((2, 25))] * 2
-    scratch += [pltpu.SemaphoreType.DMA((2, ny))] * 2 + [pltpu.SemaphoreType.DMA((2, nx))] * 2
+    scratch += [pltpu.SemaphoreType.DMA((2, 8))] * 3 + [pltpu.SemaphoreType.DMA((2,))] * 7
 
     def on_device(*args):
         vmem, smem = pl.BlockSpec(memory_space=pltpu.VMEM), pl.BlockSpec(memory_space=pltpu.SMEM)

time: 94.5 us -> 66 us (0.70)
  Pallas kernels: 92.6 us -> 64.1 us
    pallas_call x1, Pallas kernels: 92.6 us -> 64.1 us  [on_device(): pl.pallas_call(body, out_shape=jax.ShapeDtypeStruct((6, 128, 128), F32),...]
where the time goes in v1:
time: 66 us; the launch traced here: 65.8 us
  Pallas kernels  64.1 us (97%)
  local copies, waits for them, and re-layouts  1.77 us (3%)
    pallas_call x1, Pallas kernels, on_device(): pl.pallas_call(body, out_shape=jax.ShapeDtypeStruct((6, 128, 128), F32),...  64.1 us
    unnamed x1, local copies, waits for them, and re-layouts  1.77 us

profile of v1, /device:TPU:1, one launch (start us, length us, event | category | flops | bytes accessed | tf_op | source)
XLA Modules:
  0.0 65.8 jit_solution(13138736431701342947)
XLA Ops:
  0.0 64.1 %vcycle.1 = f32[6,128,128]{2,1,0:T(8,128)} custom-call(f32[6,128,128]{2,1,0:T(8,128)} %refs_0_.1, s32[6,128,128]{2,1,0:T(8,128)} %refs_1_.1, s32[8,8]{1,0:T(8,128)} %refs_2_.1, f32[8]{0:T(128)} %refs_3_.1, f32[8]{0:T(128)} %refs_4_.1, f32[8]{0:T(128)} %refs_5_.1, f32[64]{0:T(128)} %refs_6_.1), custom_call_target="tpu_custom_call" | custom-call | tf_op jit(solution)/shard_map/vcycle/pallas_call | solution.py:805
  64.1 1.8 %copy.9 = f32[6,128,128]{2,1,0:T(8,128)} copy(f32[6,128,128]{2,1,0:T(8,128)} %vcycle.1) | data formatting | bytes 786432

commit v2 on v1

--- a/solution.py
+++ b/solution.py
@@ -68,18 +68,18 @@
     return here, far, left, right
 
 
-def candidate(lv, s, t, c, k, r, n):
+def coupled(lv, s, t, c, k, r, n):
     o = 1 - c
     cf = s["cf"][t]
     here, far, left, right = around(s["u"], t, o, k, r, n, c)
     rows = pl.ds(r, n)
     a = cf[c, 0, k, rows, :] * here + cf[c, 1, k, rows, :] * far
-    b = cf[c, 2, k, rows, :] * left + cf[c, 3, k, rows, :] * right
+    a = a + cf[c, 2, k, rows, :] * left + cf[c, 3, k, rows, :] * right
     if k > 0:
         a = a + cf[c, 4, k, rows, :] * s["u"][t][o, k - 1, rows, :]
     if k < NL - 1:
-        b = b + cf[c, 5, k, rows, :] * s["u"][t][o, k + 1, rows, :]
-    return a + b
+        a = a + cf[c, 5, k, rows, :] * s["u"][t][o, k + 1, rows, :]
+    return a
 
 
 def half_sweep(lv, s, c):
@@ -87,7 +87,8 @@
         for k in range(NL):
             for r, n in lv.chunks:
                 rows = pl.ds(r, n)
-                s["u"][t][c, k, rows, :] = s["cf"][t][c, 6, k, rows, :] + candidate(lv, s, t, c, k, r, n)
+                f = s["cf"][t][c, 6, k, rows, :] + coupled(lv, s, t, c, k, r, n)
+                s["u"][t][c, k, rows, :] = f * s["iv"][t][c, k, rows, :]
 
 
 def smooth(lv, s):
@@ -103,8 +104,8 @@
     rows = pl.ds(r, n)
     parts = []
     for c in (0, 1):
-        new = s["cf"][t][c, 6, k, rows, :] + candidate(lv, s, t, c, k, r, n)
-        parts.append(s["dg"][t][c, k, rows, :] * (new - s["u"][t][c, k, rows, :]))
+        image = s["dg"][t][c, k, rows, :] * s["u"][t][c, k, rows, :] - coupled(lv, s, t, c, k, r, n)
+        parts.append(s["cf"][t][c, 6, k, rows, :] - image)
     return parts[0] + parts[1]
 
 
@@ -137,7 +138,9 @@
                 for k in range(NL):
                     own = co[t][c, 0, k, rows, :]
                     ws = [h * (own + x) for x in around(co, t, o, k, r, n, c, (0,))]
-                    diag = co[t][c, 2, k, rows, :] + ((ws[0] + ws[1]) + (ws[2] + ws[3]))
+                    m = odd(n, k, c)
+                    diag = co[t][c, 2, k, rows, :] + jnp.where(m, ws[0], ws[1]) + jnp.where(m, ws[1], ws[0])
+                    diag = diag + ws[2] + ws[3]
                     mine = co[t][c, 1, k, rows, :]
                     for other, there in ((k - 1, k > 0), (k + 1, k < NL - 1)):
                         if there:
@@ -149,7 +152,7 @@
                     inv = jnp.where(ok, 1.0 / diag, 0.0)
                     for i, w in enumerate(ws):
                         if w is not None:
-                            s["cf"][t][c, i, k, rows, :] = w * inv
+                            s["cf"][t][c, i, k, rows, :] = w
                     s["dg"][t][c, k, rows, :] = diag
                     s["iv"][t][c, k, rows, :] = inv
 
@@ -177,7 +180,7 @@
             rows = pl.ds(r, n)
             for c in (0, 1):
                 f = jnp.where(odd(n, k, c), other, even)
-                s["cf"][0][c, 6, k, rows, :] = s["iv"][0][c, k, rows, :] * f
+                s["cf"][0][c, 6, k, rows, :] = f
 
 
 def restrict_rhs(lv, s, dst):
@@ -257,7 +260,7 @@
         for c, k, r, n in cells:
             rows = pl.ds(r, n)
             z = u[c, k, rows, :]
-            w = dg[c, k, rows, :] * (z - candidate(lv, s, 0, c, k, r, n))
+            w = dg[c, k, rows, :] * z - coupled(lv, s, 0, c, k, r, n)
             ws.append(w)
             rz.append(r_ref[c, k, rows, :] * z)
             zw.append(z * w)
@@ -265,9 +268,9 @@
 
     for c, k, r, n in cells:
         rows = pl.ds(r, n)
-        z = cf[c, 6, k, rows, :]
-        u[c, k, rows, :] = z
-        r_ref[c, k, rows, :] = dg[c, k, rows, :] * z
+        f = cf[c, 6, k, rows, :]
+        r_ref[c, k, rows, :] = f
+        u[c, k, rows, :] = f * iv[c, k, rows, :]
     ws, rz, zw = images()
     for (c, k, r, n), w in zip(cells, ws):
         rows = pl.ds(r, n)
@@ -324,7 +327,7 @@
     b3c, g3c, b3f, g3f = (next(it) for _ in range(4))
     a5c, h5c, d5c, l5c = (next(it) for _ in range(4))
     a5f, h5f, d5f, l5f = (next(it) for _ in range(4))
-    s0, s1c, s1f, s3c, s3f, s5c, s5f, s6c, s6f, s7c = (next(it) for _ in range(10))
+    s0, s1c, s1f, s3c, s3f, s5c, s5f, s6c, s6f, s7c, s4c = (next(it) for _ in range(11))
 
     def exists(dx, dy):
         return (gx + dx >= 0) & (gx + dx < nx) & (gy + dy >= 0) & (gy + dy < ny)
@@ -498,6 +501,12 @@
                 total = jnp.where((lanes(16) >> 4) == k, z, total)
             dst[m] = total
 
+    def wait_for(at, size, part, sem):
+        for n in (2, 3, 4):
+            @pl.when(reach(at, size) == n)
+            def _(n=n):
+                pltpu.make_async_copy(part(n), part(n), sem).wait()
+
     def near(action, src, dst, sems):
         if action == "start":
             for q in [q for q in range(25) if q != 12]:
@@ -587,6 +596,15 @@
     pack3(cu3, 3, b3c)
     absent1(rc1, qc1, nc1)
     line("start", "gy", gy, ny, a5c, h5c, s5c)
+    for dy in (-1, 1, -2, 2):
+        @pl.when(exists(0, dy))
+        def _(dy=dy):
+            pltpu.make_async_remote_copy(
+                src_ref=b3c, dst_ref=g3c.at[12 - dy], send_sem=s3c.at[0], recv_sem=s3c.at[1],
+                device_id={"gy": gy + dy}, device_id_type=MESH,
+            ).start()
+
+    g3c[12] = b3c[...]
     h5c[gy] = a5c[...]
 
     for lv, s in zip(levels, st):
@@ -597,18 +615,10 @@
         for r in (8, 80, 88):
             sp[k, pl.ds(r, 8), :] = jnp.zeros((8, 128), F32)
 
-    arrive(ex0, s0)
-
-    for a in range(13):
-        for g in range(16):
-            uh[a, pl.ds(8 + 8 * g, 8), :] = roll(jnp.where(slot8 == g, r0[1, a], r0[0, a]), -8 * g)
-    for i, r in ((0, 0), (1, 136)):
-        for a in range(13):
-            uh[a, pl.ds(r, 8), :] = roll(jnp.where(slot8 == a, q0[2 * i + 1], q0[2 * i]), -8 * a)
-
     lv, s = levels[0], st[0]
-    for t, src in enumerate((ui, uh)):
-        for r, n in lv.chunks:
+
+    def pack0(t, src, chunks):
+        for r, n in chunks:
             ok = inside(lv, t, r, n, *place)
             rows = pl.ds(r, n)
             for k in range(NL):
@@ -621,6 +631,19 @@
                     s["co"][t][c, 0, k, rows, :] = jnp.where(ok, choose(kind, tables[0]), 0.0)
                     s["co"][t][c, 1, k, rows, :] = choose(kind, tables[1])
                     s["co"][t][c, 2, k, rows, :] = choose(kind, tables[2])
+
+    pack0(0, ui, [(16, 24), (40, 24), (64, 8)])
+    arrive(ex0, s0)
+
+    for a in range(13):
+        for g in range(16):
+            uh[a, pl.ds(8 + 8 * g, 8), :] = roll(jnp.where(slot8 == g, r0[1, a], r0[0, a]), -8 * g)
+    for i, r in ((0, 0), (1, 136)):
+        for a in range(13):
+            uh[a, pl.ds(r, 8), :] = roll(jnp.where(slot8 == a, q0[2 * i + 1], q0[2 * i]), -8 * a)
+
+    pack0(0, ui, [(8, 8), (72, 8)])
+    pack0(1, uh, lv.chunks)
     weigh(lv, s, place)
     for t, src in enumerate((ui, uh)):
         for r, n in lv.chunks:
@@ -631,7 +654,7 @@
                     f = s["co"][t][c, 2, k, rows, :] * s["u"][t][c, k, rows, :]
                     if k == 0:
                         f = f + jnp.where(odd(n, k, c), heat[1], heat[0])
-                    s["cf"][t][c, 6, k, rows, :] = s["iv"][t][c, k, rows, :] * f
+                    s["cf"][t][c, 6, k, rows, :] = f
     smooth(lv, s)
     restrict_rhs(lv, s, sr)
     for k in range(NL):
@@ -640,7 +663,15 @@
     pack1(f5, 6, mf1, kf1, rr_f1)
     exf1 = exchange1(mf1, kf1, rr_f1, rf1, qf1, nf1)
     sides(exf1, s1f, "start")
-    g3c[12] = b3c[...]
+    wait_for(gy, ny, lambda n: g3c.at[pl.ds(0, n)], s3c.at[1])
+    for dx in (-1, 1, -2, 2):
+        @pl.when(exists(dx, 0))
+        def _(dx=dx):
+            pltpu.make_async_remote_copy(
+                src_ref=g3c.at[pl.ds(10, 5)], dst_ref=g3c.at[pl.ds(10 - 5 * dx, 5)], send_sem=s4c.at[0],
+                recv_sem=s4c.at[1], device_id={"gx": gx + dx}, device_id_type=MESH,
+            ).start()
+
     absent1(rf1, qf1, nf1)
 
     arrive(exc1, s1c)
@@ -658,7 +689,6 @@
     restrict_coefficients(levels[1], st[1], c1)
     pack_coefficients(levels[2], st[2], c1, levels[1].base + 2 * (8 - levels[2].base))
     weigh(levels[2], st[2], place)
-    near("start", b3c, g3c, s3c)
 
     arrive(exf1, s1f)
     unpack1(f5, f1, 6, rf1, qf1, nf1)
@@ -671,7 +701,7 @@
     for k in range(NL):
         f3[k, pl.ds(0, 16), :] = sr[k, pl.ds(levels[2].base, 16), :]
     pack3(f3, 1, b3f)
-    near("arrive", b3c, g3c, s3c)
+    wait_for(gx, nx, lambda n: g3c.at[pl.ds(0, 5 * n)], s4c.at[1])
     near("start", b3f, g3f, s3f)
     strips = l5c.at[pl.ds(0, half - 1)]
     pltpu.make_async_copy(strips, strips, s6c.at[1]).wait()
@@ -718,7 +748,8 @@
     sides(ex0, s0, "sent")
     sides(exc1, s1c, "sent")
     sides(exf1, s1f, "sent")
-    near("sent", b3c, g3c, s3c)
+    wait_for(gy, ny, lambda n: g3c.at[pl.ds(0, n)], s3c.at[0])
+    wait_for(gx, nx, lambda n: g3c.at[pl.ds(0, 5 * n)], s4c.at[0])
     near("sent", b3f, g3f, s3f)
     line("sent", "gy", gy, ny, a5c, h5c, s5c)
     line("sent", "gy", gy, ny, a5f, h5f, s5f)
@@ -794,7 +825,7 @@
     scratch += [buffer(3, 16, 128), buffer(25, 3, 16, 128), buffer(1, 16, 128), buffer(25, 1, 16, 128)]
     for rows in (40, 16):
         scratch += [buffer(8, 128), buffer(ny, 8, 128), buffer(rows, 128), buffer(nx, rows, 128)]
-    scratch += [pltpu.SemaphoreType.DMA((2, 8))] * 3 + [pltpu.SemaphoreType.DMA((2,))] * 7
+    scratch += [pltpu.SemaphoreType.DMA((2, 8))] * 3 + [pltpu.SemaphoreType.DMA((2,))] * 8
 
     def on_device(*args):
         vmem, smem = pl.BlockSpec(memory_space=pltpu.VMEM), pl.BlockSpec(memory_space=pltpu.SMEM)

time: 66 us -> 63.2 us (0.958)
  Pallas kernels: 64.1 us -> 61.2 us
    pallas_call x1, Pallas kernels: 64.1 us -> 61.2 us  [on_device(): pl.pallas_call(body, out_shape=jax.ShapeDtypeStruct((6, 128, 128), F32),...]
where the time goes in v2:
time: 63.2 us; the launch traced here: 63 us
  Pallas kernels  61.2 us (97%)
  local copies, waits for them, and re-layouts  1.77 us (3%)
    pallas_call x1, Pallas kernels, on_device(): pl.pallas_call(body, out_shape=jax.ShapeDtypeStruct((6, 128, 128), F32),...  61.2 us
    unnamed x1, local copies, waits for them, and re-layouts  1.77 us

profile of v2, /device:TPU:1, one launch (start us, length us, event | category | flops | bytes accessed | tf_op | source)
XLA Modules:
  0.0 63.0 jit_solution(1372521115340184311)
XLA Ops:
  0.0 61.2 %vcycle.1 = f32[6,128,128]{2,1,0:T(8,128)} custom-call(f32[6,128,128]{2,1,0:T(8,128)} %refs_0_.1, s32[6,128,128]{2,1,0:T(8,128)} %refs_1_.1, s32[8,8]{1,0:T(8,128)} %refs_2_.1, f32[8]{0:T(128)} %refs_3_.1, f32[8]{0:T(128)} %refs_4_.1, f32[8]{0:T(128)} %refs_5_.1, f32[64]{0:T(128)} %refs_6_.1), custom_call_target="tpu_custom_call" | custom-call | tf_op jit(solution)/shard_map/vcycle/pallas_call | solution.py:836
  61.3 1.8 %copy.9 = f32[6,128,128]{2,1,0:T(8,128)} copy(f32[6,128,128]{2,1,0:T(8,128)} %vcycle.1) | data formatting | bytes 786432

commit v3 on v2

--- a/solution.py
+++ b/solution.py
@@ -82,19 +82,19 @@
     return a
 
 
-def half_sweep(lv, s, c):
+def half_sweep(lv, s, c, chunks):
     for t in range(len(s["u"])):
         for k in range(NL):
-            for r, n in lv.chunks:
+            for r, n in chunks:
                 rows = pl.ds(r, n)
                 f = s["cf"][t][c, 6, k, rows, :] + coupled(lv, s, t, c, k, r, n)
                 s["u"][t][c, k, rows, :] = f * s["iv"][t][c, k, rows, :]
 
 
-def smooth(lv, s):
+def smooth(lv, s, chunks=None):
     def sweep(i, _):
-        half_sweep(lv, s, 0)
-        half_sweep(lv, s, 1)
+        half_sweep(lv, s, 0, chunks or lv.chunks)
+        half_sweep(lv, s, 1, chunks or lv.chunks)
         return 0
 
     lax.fori_loop(0, 2, sweep, 0)
@@ -208,9 +208,9 @@
             dst[k, pl.ds(2 * r + 1, n, stride=2), :] = jnp.where(m, red, black)
 
 
-def correct(lv, s, src, start):
-    for k in range(NL):
-        for r, n in lv.chunks:
+def correct(lv, s, src, start, chunks=None):
+    for k in range(NL):
+        for r, n in chunks or lv.chunks:
             x = src[k, pl.ds(start + r - 8, n), :]
             rows = pl.ds(r, n)
             for t in range(len(s["u"])):
@@ -701,26 +701,26 @@
     for k in range(NL):
         f3[k, pl.ds(0, 16), :] = sr[k, pl.ds(levels[2].base, 16), :]
     pack3(f3, 1, b3f)
+    sides(ex0, s0, "sent")
+    near("start", b3f, g3f, s3f)
+    g3f[12] = b3f[...]
     wait_for(gx, nx, lambda n: g3c.at[pl.ds(0, 5 * n)], s4c.at[1])
-    near("start", b3f, g3f, s3f)
+    unpack3(b3c, g3c, 3, c3)
+    pack_coefficients(levels[3], st[3], c3, 0)
+    weigh(levels[3], st[3], place)
+    restrict_coefficients(levels[3], st[3], c1)
+    pack_coefficients(levels[4], st[4], c1, levels[3].base + 2 * (8 - levels[4].base))
+    weigh(levels[4], st[4], place)
+
+    near("arrive", b3f, g3f, s3f)
     strips = l5c.at[pl.ds(0, half - 1)]
     pltpu.make_async_copy(strips, strips, s6c.at[1]).wait()
-    pltpu.make_async_copy(strips, strips, s6c.at[0]).wait()
     mine = l5c.at[pl.ds(core * half, half)]
     relay = pltpu.make_async_remote_copy(
         src_ref=mine, dst_ref=mine, send_sem=s7c.at[0], recv_sem=s7c.at[1],
         device_id={"gx": gx + 1 - 2 * core}, device_id_type=MESH,
     )
     relay.start()
-    g3f[12] = b3f[...]
-    unpack3(b3c, g3c, 3, c3)
-    pack_coefficients(levels[3], st[3], c3, 0)
-    weigh(levels[3], st[3], place)
-    restrict_coefficients(levels[3], st[3], c1)
-    pack_coefficients(levels[4], st[4], c1, levels[3].base + 2 * (8 - levels[4].base))
-    weigh(levels[4], st[4], place)
-
-    near("arrive", b3f, g3f, s3f)
     unpack3(b3f, g3f, 1, f3)
     pack_rhs(levels[3], st[3], f3, 0)
     smooth(levels[3], st[3])
@@ -731,6 +731,7 @@
     for k in range(NL):
         cu5[k, pl.ds(0, 8), :] = sr[k, pl.ds(levels[4].base, 8), :]
     pack5(cu5, 6, a5f)
+    sides(exc1, s1c, "sent")
     line("start", "gy", gy, ny, a5f, h5f, s5f)
     h5f[gy] = a5f[...]
     relay.wait_recv()
@@ -740,14 +741,13 @@
     weigh(levels[5], st[5], place)
     line("arrive", "gy", gy, ny, a5f, h5f, s5f)
     strip5(h5f, 6, d5f)
+    sides(exf1, s1f, "sent")
     line("start", "gx", gx, nx, d5f, l5f, s6f)
     l5f[gx] = d5f[...]
     restrict_coefficients(levels[5], st[5], c1)
     pack_coefficients(levels[6], st[6], c1, 8)
     weigh(levels[6], st[6], place)
-    sides(ex0, s0, "sent")
-    sides(exc1, s1c, "sent")
-    sides(exf1, s1f, "sent")
+    pltpu.make_async_copy(strips, strips, s6c.at[0]).wait()
     wait_for(gy, ny, lambda n: g3c.at[pl.ds(0, n)], s3c.at[0])
     wait_for(gx, nx, lambda n: g3c.at[pl.ds(0, 5 * n)], s4c.at[0])
     near("sent", b3f, g3f, s3f)
@@ -774,11 +774,12 @@
         for c in (0, 1):
             rows = pl.ds(8, lv.rows)
             s["u"][0][c, k, rows, :] = s["u"][0][c, k, rows, :] + add
-    smooth(lv, s)
+    smooth(lv, s, [(8, 16)])
     for i in (3, 2, 1, 0):
+        rows = {3: [(16, 24)], 1: [(16, 24), (40, 24)]}.get(i)
         spread(levels[i + 1], st[i + 1], sp)
-        correct(levels[i], st[i], sp, 2 * levels[i + 1].base + 8 - levels[i].base)
-        smooth(levels[i], st[i])
+        correct(levels[i], st[i], sp, 2 * levels[i + 1].base + 8 - levels[i].base, rows)
+        smooth(levels[i], st[i], rows)
     u = st[0]["u"][0]
     for k in range(NL):
         for r in range(0, 64, 32):

time: 63.2 us -> 61.7 us (0.976)
  Pallas kernels: 61.2 us -> 59.8 us
    pallas_call x1, Pallas kernels: 61.2 us -> 59.8 us  [on_device(): pl.pallas_call(body, out_shape=jax.ShapeDtypeStruct((6, 128, 128), F32),...]
where the time goes in v3:
time: 61.7 us; the launch traced here: 61.6 us
  Pallas kernels  59.8 us (97%)
  local copies, waits for them, and re-layouts  1.77 us (3%)
    pallas_call x1, Pallas kernels, on_device(): pl.pallas_call(body, out_shape=jax.ShapeDtypeStruct((6, 128, 128), F32),...  59.8 us
    unnamed x1, local copies, waits for them, and re-layouts  1.77 us

profile of v3, /device:TPU:1, one launch (start us, length us, event | category | flops | bytes accessed | tf_op | source)
XLA Modules:
  0.0 61.6 jit_solution(4688180248485876788)
XLA Ops:
  0.0 59.8 %vcycle.1 = f32[6,128,128]{2,1,0:T(8,128)} custom-call(f32[6,128,128]{2,1,0:T(8,128)} %refs_0_.1, s32[6,128,128]{2,1,0:T(8,128)} %refs_1_.1, s32[8,8]{1,0:T(8,128)} %refs_2_.1, f32[8]{0:T(128)} %refs_3_.1, f32[8]{0:T(128)} %refs_4_.1, f32[8]{0:T(128)} %refs_5_.1, f32[64]{0:T(128)} %refs_6_.1), custom_call_target="tpu_custom_call" | custom-call | tf_op jit(solution)/shard_map/vcycle/pallas_call | solution.py:837
  59.8 1.8 %copy.9 = f32[6,128,128]{2,1,0:T(8,128)} copy(f32[6,128,128]{2,1,0:T(8,128)} %vcycle.1) | data formatting | bytes 786432
